TPU v7x, 32 devices: a whole 2x2x4 slice. The times are simulated.
32 devices in a mesh: ep: 2 (over core), fsdp: 16 (over z, y, x).
Axes of the slice: x: 2, y: 2, z: 4, core: 2. Of those that a mesh axis runs over, the one named last changes fastest.
Arguments:
- train_down: float32 [8, 14336, 4096], P('ep', None, 'fsdp'), may hold values from -0.0625 to 0.0625
- router_weight: float32 [4096, 8], P('fsdp', 'ep'), may hold values from -0.09375 to 0.09375
- router_gain: float32 [4096], P('fsdp'), may hold values from 0.25 to 1.75
Outputs:
- ready_down: bfloat16 [8, 14336, 4096], P('ep', 'fsdp')
- scale_down: float32 [8, 14336], P('ep', 'fsdp')
- serve_router: bfloat16 [4096, 8], replicated
All inputs are finite; a program needn't handle non-finite values.
Results may differ from a plain program's by a relative error of at most 0.001.
Values may be sent and summed in bfloat16 or wider, within the bound.
A program may use at most 192 MiB of HBM per device.

v0:
```python
import jax
import jax.numpy as jnp
from jax import lax
from jax.sharding import PartitionSpec as P


def body(train_down, router_weight, router_gain):
    total_down = lax.psum(jnp.sum(train_down * train_down, axis=2), "fsdp")
    scale_down = jnp.sqrt(total_down)
    narrow_down = (train_down / jnp.expand_dims(scale_down, 2)).astype(jnp.bfloat16)
    ready_down = lax.all_to_all(narrow_down, "fsdp", split_axis=1, concat_axis=2, tiled=True)
    scale_down = lax.dynamic_slice_in_dim(
        scale_down, lax.axis_index("fsdp") * ready_down.shape[1], ready_down.shape[1], axis=1
    )
    part_router = (router_weight * router_gain[:, None]).astype(jnp.bfloat16)
    row_router = lax.all_gather(part_router, "fsdp", axis=0, tiled=True)
    serve_router = lax.all_gather(row_router, "ep", axis=1, tiled=True)
    return (ready_down, scale_down, serve_router)


def solution(mesh):
    placed = (P("ep", None, "fsdp"), P("fsdp", "ep"), P("fsdp"))
    return jax.shard_map(
        body,
        mesh=mesh,
        in_specs=placed,
        out_specs=(P("ep", "fsdp", None), P("ep", "fsdp"), P()),
        check_vma=False,
    )
```

profile of v0, /device:TPU:11, one launch (start us, length us, event | category | flops | bytes accessed | tf_op | source)
XLA Modules:
  0.0 972.7 jit_solution(4918430820290216060)
XLA Ops:
  7.2 0.0 all-reduce.2.cloned.1.call-start
  7.2 19.4 %multiply_reduce_fusion = f32[4,14336]{1,0:T(4,128)} fusion(f32[4,14336,256]{2,1,0:T(8,128)} %param.3), kind=kLoop, calls=%fused_computation.1 | loop fusion | flops 29302784 | bytes 58949632 | tf_op jit(solution)/shard_map/reduce_sum | solution.py:8
  26.6 0.0 all-reduce.2.cloned.1.call-update
  26.7 106.3 %all-reduce.2.cloned.1.call-done = f32[4,14336]{1,0:T(4,128)} async-done(((f32[4,14336]{1,0:T(4,128)}), f32[4,14336]{1,0:T(4,128)}) %all-reduce.2.cloned.1.call-update) | async-done | bytes 229392 | tf_op jit(solution)/shard_map/psum | solution.py:8
  132.9 1.0 sqrt.3
  134.0 4.7 copy.7
  138.6 0.0 copy-start
  138.6 0.0 copy-start.1
  138.6 65.1 %fusion = bf16[4,14336,256]{2,0,1:T(4,128)(2,1)} fusion(f32[4,14336,256]{2,1,0:T(8,128)} %param.3, f32[4,14336]{0,1:T(8,128)} %copy.7), kind=kLoop, calls=%fused_computation.2 | loop fusion | flops 29360128 | bytes 88309760 | tf_op jit(solution)/shard_map/convert_element_type | solution.py:10
  203.8 6.1 all-to-all-start
  209.9 0.0 copy-done
  209.9 0.0 copy-done.1
  209.9 672.0 %all_gather.6 = bf16[4096,4]{0,1:T(4,128)(2,1)S(1)} all-gather(bf16[256,4]{0,1:T(4,128)(2,1)S(1)} %multiply_convert_fusion), channel_id=1, replica_groups=mesh['ep'=2,'fsdp'=16] {'fsdp'}, dimensions={0}, use_global_device_ids=true | all-gather | bytes 34816 | tf_op jit(solution)/shard_map/all_gather | solution.py:16
  881.9 11.4 %all-gather = bf16[2,4,4096]{2,1,0:T(4,128)(2,1)S(1)} all-gather(bf16[1,4,4096]{2,1,0:T(4,128)(2,1)S(1)} %bitcast.9), channel_id=1, replica_groups=mesh['ep'=2,'fsdp'=16] {'ep'}, dimensions={0}, use_global_device_ids=true | all-gather | bytes 98304 | tf_op jit(solution)/shard_map/all_gather | solution.py:17
  893.3 0.7 reshape.9
  894.0 0.6 constant_dynamic-slice_fusion
  894.6 0.0 all-to-all-done
  894.6 27.5 %copy.9 = bf16[4,896,16,256]{3,2,1,0:T(8,128)(2,1)} copy(bf16[4,896,16,256]{3,0,1,2:T(4,128)(2,1)} %bitcast.1) | data formatting | bytes 58720256 | tf_op jit(solution)/shard_map/all_to_all | solution.py:11
  922.1 43.7 %all_to_all.16 = bf16[4,896,4096]{2,1,0:T(8,128)(2,1)} reshape(bf16[4,896,16,256]{3,2,1,0:T(8,128)(2,1)} %copy.9) | data formatting | bytes 58720256 | tf_op jit(solution)/shard_map/all_to_all | solution.py:11
  (1 shorter events, 0.0 us)
Async XLA Ops:
  7.2 125.8 %all-reduce.2.cloned.1.call-start = ((), (), s32[]{:S(2)}) async-start(), calls=%async_computation.1 | async-start | bytes 458752 | tf_op jit(solution)/shard_map/psum | solution.py:8
  138.6 71.3 %copy-start = (f32[256,4]{0,1:T(4,128)S(1)}, f32[256,4]{0,1:T(4,128)}, u32[]{:S(2)}) copy-start(f32[256,4]{0,1:T(4,128)} %param.4) | copy-start | bytes 12292
  138.6 71.3 %copy-start.1 = (f32[256]{0:T(256)S(1)}, f32[256]{0:T(256)}, u32[]{:S(2)}) copy-start(f32[256]{0:T(256)} %param.5) | copy-start | bytes 3076
  203.8 690.8 %all-to-all-start = ((bf16[4,14336,256]{2,0,1:T(4,128)(2,1)}), bf16[4,14336,256]{2,0,1:T(4,128)(2,1)}, u32[]{:S(2)}, u32[]{:S(2)}) async-start(bf16[4,14336,256]{2,0,1:T(4,128)(2,1)} %fusion), calls=%async_computation | async-start | bytes 58720256 | tf_op jit(solution)/shard_map/all_to_all | solution.py:11
Sparse Core Ops, SparseCore 0:
  26.8 106.1 all-reduce.1
where the time goes:
time: 974 us; the launch traced here: 973 us
  blocking collectives  683 us (70%)
  waiting for transfers between devices  106 us (11%)
  other arithmetic  84.6 us (9%)
  local copies, waits for them, and re-layouts  78.2 us (8%)
  between operations  14.1 us (1%)
    all_gather x1, blocking collectives, body(): row_router = lax.all_gather(part_router, 'fsdp', axis=0, tiled=True)  672 us
    psum x1, waiting for transfers between devices, body(): total_down = lax.psum(jnp.sum(train_down * train_down, axis=2), 'fsdp')  106 us
    all_to_all x2, local copies, waits for them, and re-layouts, body(): lax.all_to_all(narrow_down, 'fsdp', split_axis=1, concat_axis=2, tiled=True)  71.2 us
    convert_element_type x1, other arithmetic, body(): (train_down / jnp.expand_dims(scale_down, 2)).astype(jnp.bfloat16)  65.1 us
  transfers between devices with their start and end apart: 2, of which 1 were waited for; matrix products, arithmetic and copies ran while one was open for 0% of the time, Pallas kernels for 0%

commit v1 on v0

--- a/solution.py
+++ b/solution.py
@@ -5,7 +5,7 @@
 
 
 def body(train_down, router_weight, router_gain):
-    total_down = lax.psum(jnp.sum(train_down * train_down, axis=2), "fsdp")
+    total_down = jnp.sum(lax.all_gather(jnp.sum(train_down * train_down, axis=2), "fsdp"), axis=0)
     scale_down = jnp.sqrt(total_down)
     narrow_down = (train_down / jnp.expand_dims(scale_down, 2)).astype(jnp.bfloat16)
     ready_down = lax.all_to_all(narrow_down, "fsdp", split_axis=1, concat_axis=2, tiled=True)

time: 974 us -> 941 us (0.966)
  waiting for transfers between devices: 106 us -> 71.6 us
    psum x1 -> x0, waiting for transfers between devices: 106 us -> none  [body(): total_down = lax.psum(jnp.sum(train_down * train_down, axis=2), 'fsdp')]
    all_gather x0 -> x1, waiting for transfers between devices: none -> 71.6 us  [body(): lax.all_gather(jnp.sum(train_down * train_down, axis=2), 'fsdp')]
    reduce_sum x1 -> x2, other arithmetic: 19.4 us -> 22.1 us  [the longest x1 19.4 us: body(): jnp.sum(train_down * train_down, axis=2)]
where the time goes in v1:
time: 941 us; the launch traced here: 939 us
  blocking collectives  684 us (73%)
  other arithmetic  87.2 us (9%)
  local copies, waits for them, and re-layouts  77.3 us (8%)
  waiting for transfers between devices  71.6 us (8%)
  between operations  14.1 us (1%)
    all_gather x1, blocking collectives, body(): row_router = lax.all_gather(part_router, 'fsdp', axis=0, tiled=True)  672 us
    all_gather x1, waiting for transfers between devices, body(): lax.all_gather(jnp.sum(train_down * train_down, axis=2), 'fsdp')  71.6 us
    all_to_all x2, local copies, waits for them, and re-layouts, body(): lax.all_to_all(narrow_down, 'fsdp', split_axis=1, concat_axis=2, tiled=True)  71.2 us
    convert_element_type x1, other arithmetic, body(): (train_down / jnp.expand_dims(scale_down, 2)).astype(jnp.bfloat16)  65.1 us
    reduce_sum x1, other arithmetic, body(): jnp.sum(train_down * train_down, axis=2)  19.4 us
  transfers between devices with their start and end apart: 2, of which 1 were waited for; matrix products, arithmetic and copies ran while one was open for 0% of the time, Pallas kernels for 0%

profile of v1, /device:TPU:11, one launch (start us, length us, event | category | flops | bytes accessed | tf_op | source)
XLA Modules:
  0.0 939.5 jit_solution(7723646013048486692)
XLA Ops:
  7.2 0.0 all-gather.5.cloned.1.call-start
  7.2 19.4 %multiply_reduce_fusion = f32[4,14336]{1,0:T(4,128)} fusion(f32[4,14336,256]{2,1,0:T(8,128)} %param.3), kind=kLoop, calls=%fused_computation.1 | loop fusion | flops 29302784 | bytes 58949632 | tf_op jit(solution)/shard_map/reduce_sum | solution.py:8
  26.6 0.0 all-gather.5.cloned.1.call-update
  26.7 71.6 %all-gather.5.cloned.1.call-done = f32[16,4,14336]{2,1,0:T(4,128)} async-done(((f32[1,4,14336]{2,1,0:T(4,128)}), f32[16,4,14336]{2,1,0:T(4,128)}) %all-gather.5.cloned.1.call-update) | async-done | bytes 3670032 | tf_op jit(solution)/shard_map/all_gather | solution.py:8
  98.3 2.6 reduce_sum.19
  100.9 0.1 sqrt.7
  101.0 4.7 copy.7
  105.7 65.1 %fusion = bf16[4,14336,256]{2,0,1:T(4,128)(2,1)} fusion(f32[4,14336,256]{2,1,0:T(8,128)} %param.3, f32[4,14336]{0,1:T(8,128)} %copy.7), kind=kLoop, calls=%fused_computation.2 | loop fusion | flops 29360128 | bytes 88309760 | tf_op jit(solution)/shard_map/convert_element_type | solution.py:10
  170.8 0.0 copy-start
  170.8 0.0 copy-start.1
  170.8 5.7 all-to-all-start
  176.5 0.0 copy-done
  176.5 0.0 copy-done.1
  176.5 672.2 %all_gather.14 = bf16[4096,4]{0,1:T(4,128)(2,1)S(1)} all-gather(bf16[256,4]{0,1:T(4,128)(2,1)S(1)} %multiply_convert_fusion), channel_id=1, replica_groups=mesh['ep'=2,'fsdp'=16] {'fsdp'}, dimensions={0}, use_global_device_ids=true | all-gather | bytes 34816 | tf_op jit(solution)/shard_map/all_gather | solution.py:16
  848.7 11.4 %all-gather.2 = bf16[2,4,4096]{2,1,0:T(4,128)(2,1)S(1)} all-gather(bf16[1,4,4096]{2,1,0:T(4,128)(2,1)S(1)} %bitcast.11), channel_id=1, replica_groups=mesh['ep'=2,'fsdp'=16] {'ep'}, dimensions={0}, use_global_device_ids=true | all-gather | bytes 98304 | tf_op jit(solution)/shard_map/all_gather | solution.py:17
  860.1 0.7 reshape.14
  860.8 0.6 constant_dynamic-slice_fusion
  861.4 0.0 all-to-all-done
  861.4 27.5 %copy.9 = bf16[4,896,16,256]{3,2,1,0:T(8,128)(2,1)} copy(bf16[4,896,16,256]{3,0,1,2:T(4,128)(2,1)} %bitcast.2) | data formatting | bytes 58720256 | tf_op jit(solution)/shard_map/all_to_all | solution.py:11
  888.9 43.7 %all_to_all.16 = bf16[4,896,4096]{2,1,0:T(8,128)(2,1)} reshape(bf16[4,896,16,256]{3,2,1,0:T(8,128)(2,1)} %copy.9) | data formatting | bytes 58720256 | tf_op jit(solution)/shard_map/all_to_all | solution.py:11
  (1 shorter events, 0.0 us)
Async XLA Ops:
  7.2 91.1 %all-gather.5.cloned.1.call-start = ((), (), s32[]{:S(2)}) async-start(), calls=%async_computation.1 | async-start | bytes 3899392 | tf_op jit(solution)/shard_map/all_gather | solution.py:8
  170.8 5.7 copy-start
  170.8 5.7 copy-start.1
  170.8 690.5 %all-to-all-start = ((bf16[4,14336,256]{2,0,1:T(4,128)(2,1)}), bf16[4,14336,256]{2,0,1:T(4,128)(2,1)}, u32[]{:S(2)}, u32[]{:S(2)}) async-start(bf16[4,14336,256]{2,0,1:T(4,128)(2,1)} %fusion), calls=%async_computation | async-start | bytes 58720256 | tf_op jit(solution)/shard_map/all_to_all | solution.py:11
Sparse Core Ops, SparseCore 0:
  26.8 71.4 all-gather.4
